TPU v7x, 32 devices: a whole 2x2x4 slice. The times are simulated.
32 devices in a mesh: tm: 16 (over z, y, core), series: 2 (over x).
Axes of the slice: x: 2, y: 2, z: 4, core: 2. Of those that a mesh axis runs over, the one named last changes fastest.
Arguments:
- history: bfloat16 [4, 4096, 1024], P('series', 'tm'), may hold values from -36 to 36
- lengths: int32 [4], P('series'), may hold values from 512 to 4096
- head_window: int32 [16], replicated, may hold values from 32 to 512, as said below
- input_proj: bfloat16 [1024, 3072], replicated
- output_proj: bfloat16 [1024, 1024], replicated, may hold values from -0.1875 to 0.1875
- mixer_down: bfloat16 [1024, 512], replicated, may hold values from -0.1875 to 0.1875
- mixer_up: bfloat16 [512, 1024], replicated, may hold values from -0.25 to 0.25
- series_mix: bfloat16 [4, 4], replicated, may hold values from -3 to 3
Outputs:
- layer_out: bfloat16 [4, 4096, 1024], P('series', 'tm')
Inputs may be any that keep to these rules, and one draw needn't show every extreme that they name: `head_window`: some head has exactly 512.
All inputs are finite; a program needn't handle non-finite values.
Results may differ from a plain program's by a relative error of at most 0.0065.
Values may be sent and summed in bfloat16 or wider, within the bound.
No kernel may reach another device: no remote copies, remote signals or barrier semaphores. Data moves between devices by JAX's collectives and lax.ppermute only.
A program may use at most 128 MiB of HBM per device.

v0:
```python
import jax
import jax.numpy as jnp
from jax import lax
from jax.sharding import PartitionSpec as P

HEADS = 16
WINDOW = 512


def from_behind(block, axis, distance):
    devices = range(lax.axis_size(axis))
    route = [(i - distance, i) for i in devices if i - distance in devices]
    return lax.ppermute(block, axis, route)


def attend_series(queries, keys_values, length, head_window, query_first, key_first, patches):
    query_rows = queries.shape[0]
    model_width = queries.shape[1]
    key_rows = keys_values.shape[0]
    head_size = model_width // HEADS
    group_heads = min(4, HEADS)
    group_count = HEADS // group_heads
    group_width = group_heads * head_size
    query_pos = query_first + jnp.arange(query_rows, dtype=jnp.int32)
    key_pos = key_first + jnp.arange(key_rows, dtype=jnp.int32)
    key_valid = (key_pos >= patches - length) & (key_pos < patches)
    distance = jnp.abs(query_pos[:, None] - key_pos[None, :])

    def per_group(group_index):
        column = group_index * group_width
        group_queries = lax.dynamic_slice_in_dim(queries, column, group_width, 1).reshape(
            query_rows, group_heads, head_size
        )
        group_keys = lax.dynamic_slice_in_dim(keys_values, column, group_width, 1).reshape(
            key_rows, group_heads, head_size
        )
        group_values = lax.dynamic_slice_in_dim(
            keys_values, model_width + column, group_width, 1
        ).reshape(key_rows, group_heads, head_size)
        reaches = lax.dynamic_slice_in_dim(head_window, group_index * group_heads, group_heads, 0)
        scores = jnp.einsum(
            "qhd,khd->hqk", group_queries, group_keys, preferred_element_type=jnp.float32
        ) * head_size ** (-0.5)
        allowed = (distance[None, :, :] <= reaches[:, None, None]) & key_valid[None, None, :]
        scores = jnp.where(allowed, scores, -1e30)
        largest = jnp.max(scores, axis=-1, keepdims=True)
        weights = jnp.exp(scores - largest)
        totals = jnp.sum(weights, axis=-1)
        probabilities = weights.astype(jnp.bfloat16)
        combined = (
            jnp.einsum(
                "hqk,khd->qhd", probabilities, group_values, preferred_element_type=jnp.float32
            )
            / jnp.transpose(totals)[:, :, None]
        )
        return combined.reshape(query_rows, group_width)

    grouped = lax.map(per_group, jnp.arange(group_count, dtype=jnp.int32))
    combined = jnp.transpose(grouped, (1, 0, 2)).reshape(query_rows, model_width)
    query_valid = query_pos >= patches - length
    return jnp.where(query_valid[:, None], combined, 0.0).astype(jnp.bfloat16)


def on_device(
    history, lengths, head_window, input_proj, output_proj, mixer_down, mixer_up, series_mix
):
    local_series, local_patches, model_width = history.shape
    packed = jnp.einsum(
        "spd,de->spe", history, input_proj, preferred_element_type=jnp.float32
    ).astype(jnp.bfloat16)
    queries = packed[:, :, :model_width]
    keys_values = packed[:, :, model_width:]
    hops_count = -(-WINDOW // local_patches)
    earlier = []
    following = []
    kv_weight = input_proj[:, model_width:]
    for offset in range(1, hops_count + 1):
        before_rows = from_behind(history, "tm", offset)
        after_rows = from_behind(history, "tm", -offset)
        earlier.insert(
            0,
            jnp.einsum(
                "spd,de->spe", before_rows, kv_weight, preferred_element_type=jnp.float32
            ).astype(jnp.bfloat16),
        )
        following.append(
            jnp.einsum(
                "spd,de->spe", after_rows, kv_weight, preferred_element_type=jnp.float32
            ).astype(jnp.bfloat16)
        )
    context = jnp.concatenate(earlier + [keys_values] + following, axis=1)
    position = lax.axis_index("tm")
    patches = local_patches * lax.axis_size("tm")
    query_first = position * local_patches
    key_first = (position - hops_count) * local_patches

    def per_series(inputs):
        series_queries, series_context, length = inputs
        return attend_series(
            series_queries, series_context, length, head_window, query_first, key_first, patches
        )

    attended = lax.map(per_series, (queries, context, lengths))
    hidden = (
        history.astype(jnp.float32)
        + jnp.einsum("spd,de->spe", attended, output_proj, preferred_element_type=jnp.float32)
    ).astype(jnp.bfloat16)
    branch = jnp.einsum(
        "spd,dc->spc", hidden, mixer_down, preferred_element_type=jnp.float32
    ).astype(jnp.bfloat16)
    series_first = lax.axis_index("series") * local_series
    own_rows = lax.dynamic_slice_in_dim(series_mix, series_first, local_series, 0)
    combined = jnp.einsum(
        "ab,bpc->apc",
        own_rows,
        lax.all_gather(branch, "series", axis=0, tiled=True),
        preferred_element_type=jnp.float32,
    )
    combined = combined.astype(jnp.bfloat16)
    update = jnp.einsum("spc,cd->spd", combined, mixer_up, preferred_element_type=jnp.float32)
    return (hidden.astype(jnp.float32) + update).astype(jnp.bfloat16)


def solution(mesh):
    in_specs = (P("series", "tm", None), P("series"), P(), P(), P(), P(), P(), P())
    out_specs = P("series", "tm", None)
    return jax.shard_map(
        on_device, mesh=mesh, in_specs=in_specs, out_specs=out_specs, check_vma=False
    )
```

profile of v0, /device:TPU:0, one launch (start us, length us, event | category | flops | bytes accessed | tf_op | source)
XLA Modules:
  0.0 253.0 jit_solution(13896051567737535328)
XLA Ops:
  6.5 6.0 %collective-permute-start = (bf16[2,256,1024]{2,1,0:T(8,128)(2,1)}, bf16[2,256,1024]{2,1,0:T(8,128)(2,1)}, u32[]{:S(2)}, u32[]{:S(2)}) collective-permute-start(bf16[2,256,1024]{2,1,0:T(8,128)(2,1)} %param.12), channel_id=1, source_target_pairs={{0,4},{2,6},{4,8},{6,10},{8,12},{10,14},{12,16},{14,18},{16,20},{1... | collective-permute-start | bytes 3145736 | tf_op jit(solution)/shard_map/ppermute | solution.py:13
  12.5 2.5 collective-permute-start.1
  17.6 6.5 %fusion.22 = bf16[2,256,3072]{2,1,0:T(8,128)(2,1)S(1)} fusion(bf16[2,256,1024]{2,1,0:T(8,128)(2,1)} %param.12, bf16[1024,3072]{1,0:T(8,128)(2,1)} %param.15), kind=kOutput, calls=%fused_computation.29 | convolution fusion | flops 3222798336 | bytes 10485760 | tf_op jit(solution)/shard_map/spd,de->spe/dot_general | solution.py:68
  26.9 42.2 %collective-permute-done = bf16[2,256,1024]{2,1,0:T(8,128)(2,1)} collective-permute-done((bf16[2,256,1024]{2,1,0:T(8,128)(2,1)}, bf16[2,256,1024]{2,1,0:T(8,128)(2,1)}, u32[]{:S(2)}, u32[]{:S(2)}) %collective-permute-start) | collective-permute-done | bytes 1048608 | tf_op jit(solution)/shard_map/ppermute | solution.py:13
  69.1 5.0 %fusion.36 = bf16[2,1280,2048]{2,1,0:T(8,128)(2,1)S(1)} fusion(bf16[2,256,1024]{2,1,0:T(8,128)(2,1)} %collective-permute-done, bf16[1024,3072]{1,0:T(8,128)(2,1)} %param.15), kind=kOutput, calls=%fused_computation.39 | convolution fusion | flops 2148532224 | bytes 7340032 | tf_op jit(solution)/shard_map/spd,de->spe/dot_general | solution.py:82
  74.2 5.0 %fusion.42 = bf16[2,1280,2048]{2,1,0:T(8,128)(2,1)S(1)} fusion(bf16[2,1280,2048]{2,1,0:T(8,128)(2,1)S(1)} %fusion.36, bf16[2,256,1024]{2,1,0:T(8,128)(2,1)} %collective-permute-done.1, bf16[1024,3072]{1,0:T(8,128)(2,1)} %param.15), kind=kOutput, calls=%fused_computation.41 | convolution fusion | flops 2148532224 | bytes 7340032 | tf_op jit(solution)/shard_map/spd,de->spe/dot_general | solution.py:82
  79.4 3.6 %fusion.48 = bf16[2,1280,2048]{2,1,0:T(8,128)(2,1)S(1)} fusion(bf16[2,1280,2048]{2,1,0:T(8,128)(2,1)S(1)} %slice_dynamic-update-slice_fusion, bf16[2,256,1024]{2,1,0:T(8,128)(2,1)} %collective-permute-done.2, bf16[1024,3072]{1,0:T(8,128)(2,1)S(1)} %bitcast.116), kind=kOutput, calls=%fused_computation.43 | convolution fusion | flops 2148532224 | bytes 7340032 | tf_op jit(solution)/shard_map/spd,de->spe/dot_general | solution.py:87
  83.0 2.3 fusion.54
  85.3 4.0 %copy-done.1 = bf16[2,1280,2048]{2,1,0:T(8,128)(2,1)} copy-done((bf16[2,1280,2048]{2,1,0:T(8,128)(2,1)}, bf16[2,1280,2048]{2,1,0:T(8,128)(2,1)S(1)}, u32[]{:S(2)}) %copy-start.1) | copy-done | bytes 10485784
  89.3 118.7 %while.33 = (s32[]{:T(128)}, bf16[2,256,1024]{1,2,0:T(8,128)(2,1)}, s32[]{:T(128)}, s32[2]{0:T(128)S(1)}, bf16[2,256,1024]{2,1,0:T(8,128)(2,1)}, /*index=5*/bf16...) while((s32[]{:T(128)}, bf16[2,256,1024]{1,2,0:T(8,128)(2,1)}, ...), condition=%wide.region_5.6_spmd, body=%wide.region_0.5_spmd.sunk | while | flops 348394496 | bytes 47223572 | solution.py:103
  90.6 5.6 %constant_dynamic-slice_fusion.9 = bf16[1,1280,2048]{2,1,0:T(8,128)(2,1)} fusion(bf16[2,1280,2048]{2,1,0:T(8,128)(2,1)} %get-tuple-element.545, s32[]{:T(128)} %get-tuple-element.521), kind=kLoop, calls=%fused_computation.25.clone.1 | loop fusion | bytes 10485764 | tf_op jit(solution)/shard_map/while/body/jit(dynamic_index_in_dim)/dynamic_slice | solution.py:103
  96.2 7.9 %copy.26 = bf16[1,1280,2048]{1,2,0:T(8,128)(2,1)} copy(bf16[1,1280,2048]{2,1,0:T(8,128)(2,1)} %constant_dynamic-slice_fusion.9) | data formatting | bytes 10485760 | tf_op jit(solution)/shard_map/while/body/jit(dynamic_index_in_dim)/dynamic_slice | solution.py:103
  106.7 40.1 %while.34 = (s32[]{:T(128)}, bf16[4,256,256]{1,2,0:T(8,128)(2,1)}, s32[4]{0:T(128)}, bf16[1280,2048]{0,1:T(8,128)(2,1)}, s32[16]{0:T(128)}, /*index=5*/bf16[256,...) while((s32[]{:T(128)}, bf16[4,256,256]{1,2,0:T(8,128)(2,1)}, ...), condition=%wide.region_4.4_spmd.clone, body=%wide.region_1.3_spmd.clone.sunk | while | flops 348130304 | bytes 23098768 | solution.py:58
  142.3 1.8 fusion.98
  146.7 1.9 fusion.92
  149.9 5.6 %constant_dynamic-slice_fusion.9 = bf16[1,1280,2048]{2,1,0:T(8,128)(2,1)} fusion(bf16[2,1280,2048]{2,1,0:T(8,128)(2,1)} %get-tuple-element.545, s32[]{:T(128)} %get-tuple-element.521), kind=kLoop, calls=%fused_computation.25.clone.1 | loop fusion | bytes 10485764 | tf_op jit(solution)/shard_map/while/body/jit(dynamic_index_in_dim)/dynamic_slice | solution.py:103
  155.5 7.9 %copy.26 = bf16[1,1280,2048]{1,2,0:T(8,128)(2,1)} copy(bf16[1,1280,2048]{2,1,0:T(8,128)(2,1)} %constant_dynamic-slice_fusion.9) | data formatting | bytes 10485760 | tf_op jit(solution)/shard_map/while/body/jit(dynamic_index_in_dim)/dynamic_slice | solution.py:103
  166.0 40.1 %while.34 = (s32[]{:T(128)}, bf16[4,256,256]{1,2,0:T(8,128)(2,1)}, s32[4]{0:T(128)}, bf16[1280,2048]{0,1:T(8,128)(2,1)}, s32[16]{0:T(128)}, /*index=5*/bf16[256,...) while((s32[]{:T(128)}, bf16[4,256,256]{1,2,0:T(8,128)(2,1)}, ...), condition=%wide.region_4.4_spmd.clone, body=%wide.region_1.3_spmd.clone.sunk | while | flops 348130304 | bytes 23098768 | solution.py:58
  201.7 1.8 fusion.98
  206.1 1.9 fusion.92
  208.0 3.0 %add_convert_fusion.1 = bf16[2,256,1024]{2,1,0:T(8,128)(2,1)S(1)} fusion(bf16[2,256,1024]{2,1,0:T(8,128)(2,1)} %param.12, bf16[2,256,1024]{1,2,0:T(8,128)(2,1)} %get-tuple-element.223, bf16[1024,1024]{1,0:T(8,128)(2,1)S(1)} %copy-done), kind=kOutput, calls=%fused_computation.54 | convolution fusion | flops 1075314688 | bytes 5242880 | tf_op jit(solution)/shard_map/spd,de->spe/dot_general | solution.py:106
  213.5 27.6 %all-gather.2.cloned.1.call-done = bf16[4,256,512]{2,1,0:T(8,128)(2,1)} async-done(((bf16[2,256,512]{2,1,0:T(8,128)(2,1)}), bf16[4,256,512]{2,1,0:T(8,128)(2,1)}) %all-gather.2.cloned.1.call-update) | async-done | bytes 1048592 | tf_op jit(solution)/shard_map/all_gather | solution.py:116
  241.1 2.1 fusion.67
  243.2 2.9 %add_convert_fusion = bf16[2,256,1024]{2,1,0:T(8,128)(2,1)} fusion(bf16[2,256,1024]{2,1,0:T(8,128)(2,1)} %copy-done.8, bf16[512,1024]{1,0:T(8,128)(2,1)S(1)} %copy-done.5, bf16[2,256,512]{2,0,1:T(2,128)(2,1)S(1)} %fusion.67), kind=kOutput, calls=%fused_computation.53 | convolution fusion | flops 538443776 | bytes 3670016 | tf_op jit(solution)/shard_map/spc,cd->spd/dot_general | solution.py:120
  (127 shorter events, 81.5 us)
Async XLA Ops:
  6.5 201.5 %copy-start = (bf16[1024,1024]{1,0:T(8,128)(2,1)S(1)}, bf16[1024,1024]{1,0:T(8,128)(2,1)}, u32[]{:S(2)}) copy-start(bf16[1024,1024]{1,0:T(8,128)(2,1)} %param.16) | copy-start | bytes 6291460
  6.5 234.5 %all-gather.2.cloned.1.call-start = ((), (), s32[]{:S(2)}) async-start(), calls=%async_computation | async-start | bytes 1572864 | tf_op jit(solution)/shard_map/all_gather | solution.py:116
  6.5 62.6 %collective-permute-start = (bf16[2,256,1024]{2,1,0:T(8,128)(2,1)}, bf16[2,256,1024]{2,1,0:T(8,128)(2,1)}, u32[]{:S(2)}, u32[]{:S(2)}) collective-permute-start(bf16[2,256,1024]{2,1,0:T(8,128)(2,1)} %param.12), channel_id=1, source_target_pairs={{0,4},{2,6},{4,8},{6,10},{8,12},{10,14},{12,16},{14,18},{16,20},{1... | collective-permute-start | bytes 3145736 | tf_op jit(solution)/shard_map/ppermute | solution.py:13
  12.5 61.6 %collective-permute-start.1 = (bf16[2,256,1024]{2,1,0:T(8,128)(2,1)}, bf16[2,256,1024]{2,1,0:T(8,128)(2,1)}, u32[]{:S(2)}, u32[]{:S(2)}) collective-permute-start(bf16[2,256,1024]{2,1,0:T(8,128)(2,1)} %param.12), channel_id=1, source_target_pairs={{0,2},{2,4},{4,6},{6,8},{8,10},{10,12},{12,14},{14,16},{16,18},{18... | collective-permute-start | bytes 3145736 | tf_op jit(solution)/shard_map/ppermute | solution.py:13
  15.0 64.3 %collective-permute-start.2 = (bf16[2,256,1024]{2,1,0:T(8,128)(2,1)}, bf16[2,256,1024]{2,1,0:T(8,128)(2,1)}, u32[]{:S(2)}, u32[]{:S(2)}) collective-permute-start(bf16[2,256,1024]{2,1,0:T(8,128)(2,1)} %param.12), channel_id=1, source_target_pairs={{2,0},{4,2},{6,4},{8,6},{10,8},{12,10},{14,12},{16,14},{18,16},{20... | collective-permute-start | bytes 3145736 | tf_op jit(solution)/shard_map/ppermute | solution.py:13
  16.3 66.7 %collective-permute-start.3 = (bf16[2,256,1024]{2,1,0:T(8,128)(2,1)}, bf16[2,256,1024]{2,1,0:T(8,128)(2,1)S(1)}, u32[]{:S(2)}, u32[]{:S(2)}) collective-permute-start(bf16[2,256,1024]{2,1,0:T(8,128)(2,1)} %param.12), channel_id=1, source_target_pairs={{4,0},{6,2},{8,4},{10,6},{12,8},{14,10},{16,12},{18,14},{20,16},{2... | collective-permute-start | bytes 3145736 | tf_op jit(solution)/shard_map/ppermute | solution.py:13
  24.2 1.6 copy-start.2
  69.1 10.2 %slice-start = ((s8[6291456]{0:T(1024)(128)(4,1)}), s8[4194304]{0:T(1024)(128)(4,1)S(1)}, s32[]{:S(2)}) async-start(s8[6291456]{0:T(1024)(128)(4,1)} %bitcast.115), calls=%async_computation.1 | async-start | bytes 8388608
  74.1 5.0 %copy-start.3 = (bf16[2,256,3072]{2,1,0:T(8,128)(2,1)S(1)}, bf16[2,256,3072]{2,1,0:T(8,128)(2,1)}, u32[]{:S(2)}) copy-start(bf16[2,256,3072]{2,1,0:T(8,128)(2,1)} %copy-done.2) | copy-start | bytes 9437188
  74.1 5.2 %slice-start.1 = ((s8[6291456]{0:T(1024)(128)(4,1)}), s8[2097152]{0:T(1024)(128)(4,1)S(1)}, s32[]{:S(2)}) async-start(s8[6291456]{0:T(1024)(128)(4,1)} %bitcast.115), calls=%async_computation.2 | async-start | bytes 4194304
  83.0 6.4 %copy-start.7 = (s32[2]{0:T(128)S(1)}, s32[2]{0:T(128)}, u32[]{:S(2)}) copy-start(s32[2]{0:T(128)} %param.13) | copy-start | bytes 28
  85.3 4.0 %copy-start.1 = (bf16[2,1280,2048]{2,1,0:T(8,128)(2,1)}, bf16[2,1280,2048]{2,1,0:T(8,128)(2,1)S(1)}, u32[]{:S(2)}) copy-start(bf16[2,1280,2048]{2,1,0:T(8,128)(2,1)S(1)} %fusion.54) | copy-start | bytes 31457284
  208.0 4.0 %copy-start.4 = (bf16[1024,512]{1,0:T(8,128)(2,1)S(1)}, bf16[1024,512]{1,0:T(8,128)(2,1)}, u32[]{:S(2)}) copy-start(bf16[1024,512]{1,0:T(8,128)(2,1)} %param.17) | copy-start | bytes 3145732
  208.0 33.1 %copy-start.6 = (bf16[4,4]{1,0:T(4,128)(2,1)S(1)}, bf16[4,4]{1,0:T(4,128)(2,1)}, u32[]{:S(2)}) copy-start(bf16[4,4]{1,0:T(4,128)(2,1)} %param.19) | copy-start | bytes 100
  208.0 35.2 %copy-start.5 = (bf16[512,1024]{1,0:T(8,128)(2,1)S(1)}, bf16[512,1024]{1,0:T(8,128)(2,1)}, u32[]{:S(2)}) copy-start(bf16[512,1024]{1,0:T(8,128)(2,1)} %param.18) | copy-start | bytes 3145732
  211.0 1.0 copy-start.8
Sparse Core Ops, SparseCore 0:
  213.6 27.3 all-gather.1
where the time goes:
time: 255 us; the launch traced here: 253 us
  local copies, waits for them, and re-layouts  80 us (31%)
  waiting for transfers between devices  69.8 us (27%)
  matrix products  54.1 us (21%)
  other arithmetic  13.6 us (5%)
  between operations  13.6 us (5%)
  starting transfers between devices  11.1 us (4%)
  loops' own time  10.8 us (4%)
    ppermute x4, waiting for transfers between devices, from_behind(): return lax.ppermute(block, axis, route)  42.3 us
    dynamic_slice x10, local copies, waits for them, and re-layouts, on_device(): attended = lax.map(per_series, (queries, context, lengths))  32.4 us
    all_gather x1, waiting for transfers between devices, on_device(): lax.all_gather(branch, 'series', axis=0, tiled=True)  27.6 us
    dot_general x8, matrix products, per_group(): jnp.einsum('qhd,khd->hqk', group_queries, group_keys, preferred_element_t...  14.1 us
    ppermute x4, starting transfers between devices, from_behind(): return lax.ppermute(block, axis, route)  11.1 us
    dynamic_slice x8, local copies, waits for them, and re-layouts, per_group(): lax.dynamic_slice_in_dim(keys_values, column, group_width, 1)  11 us
    dot_general x2, matrix products, on_device(): jnp.einsum('spd,de->spe', before_rows, kv_weight, preferred_element_type=...  9.98 us
    another operation x2, loops' own time, attend_series(): grouped = lax.map(per_group, jnp.arange(group_count, dtype=jnp.int32))  9.47 us
  transfers between devices with their start and end apart: 5, of which 2 were waited for; matrix products, arithmetic and copies ran while one was open for 8% of the time, Pallas kernels for 0%

commit v1 on v0

--- a/solution.py
+++ b/solution.py
@@ -110,12 +110,19 @@
     ).astype(jnp.bfloat16)
     series_first = lax.axis_index("series") * local_series
     own_rows = lax.dynamic_slice_in_dim(series_mix, series_first, local_series, 0)
-    combined = jnp.einsum(
-        "ab,bpc->apc",
-        own_rows,
-        lax.all_gather(branch, "series", axis=0, tiled=True),
-        preferred_element_type=jnp.float32,
-    )
+    size, index, rows = (lax.axis_size("series"), lax.axis_index("series"), branch.shape[0])
+    upward = [(i_2, (i_2 + 1) % size) for i_2 in range(size)]
+    held, combined = (branch, None)
+    for step in range(size):
+        arriving = lax.ppermute(held, "series", upward) if step < size - 1 else None
+        absorb = jnp.einsum(
+            "ab,bpc->apc",
+            lax.dynamic_slice_in_dim(own_rows, (index - step) % size * rows, held.shape[0], axis=1),
+            held,
+            preferred_element_type=jnp.float32,
+        )
+        combined = absorb if combined is None else combined + absorb
+        held = arriving
     combined = combined.astype(jnp.bfloat16)
     update = jnp.einsum("spc,cd->spd", combined, mixer_up, preferred_element_type=jnp.float32)
     return (hidden.astype(jnp.float32) + update).astype(jnp.bfloat16)

time: 255 us -> 231 us (0.906)
  the two profiles are of different devices: /device:TPU:0 before, /device:TPU:1 now
where the time goes in v1:
time: 231 us; the launch traced here: 229 us
  local copies, waits for them, and re-layouts  81.4 us (35%)
  matrix products  55.5 us (24%)
  waiting for transfers between devices  53.1 us (23%)
  other arithmetic  13.6 us (6%)
  starting transfers between devices  12.9 us (6%)
  loops' own time  12.4 us (5%)
    ppermute x4, waiting for transfers between devices, from_behind(): return lax.ppermute(block, axis, route)  46.3 us
    dynamic_slice x10, local copies, waits for them, and re-layouts, on_device(): attended = lax.map(per_series, (queries, context, lengths))  32.3 us
    dot_general x8, matrix products, per_group(): jnp.einsum('qhd,khd->hqk', group_queries, group_keys, preferred_element_t...  14.2 us
    ppermute x4, starting transfers between devices, from_behind(): return lax.ppermute(block, axis, route)  11.7 us
    another operation x2, loops' own time, attend_series(): grouped = lax.map(per_group, jnp.arange(group_count, dtype=jnp.int32))  11.3 us
    dynamic_slice x8, local copies, waits for them, and re-layouts, per_group(): lax.dynamic_slice_in_dim(keys_values, column, group_width, 1)  11 us
    dynamic_slice x8, local copies, waits for them, and re-layouts, attend_series(): grouped = lax.map(per_group, jnp.arange(group_count, dtype=jnp.int32))  10.5 us
    dot_general x2, matrix products, on_device(): jnp.einsum('spd,de->spe', before_rows, kv_weight, preferred_element_type=...  9.83 us
  transfers between devices with their start and end apart: 5, of which 3 were waited for; matrix products, arithmetic and copies ran while one was open for 10% of the time, Pallas kernels for 0%

profile of v1, /device:TPU:1, one launch (start us, length us, event | category | flops | bytes accessed | tf_op | source)
XLA Modules:
  0.0 229.2 jit_solution(18353838745938396333)
XLA Ops:
  0.0 5.1 %collective-permute-start = (bf16[2,256,1024]{2,1,0:T(8,128)(2,1)}, bf16[2,256,1024]{2,1,0:T(8,128)(2,1)}, u32[]{:S(2)}, u32[]{:S(2)}) collective-permute-start(bf16[2,256,1024]{2,1,0:T(8,128)(2,1)} %param.12), channel_id=1, source_target_pairs={{0,4},{2,6},{4,8},{6,10},{8,12},{10,14},{12,16},{14,18},{16,20},{1... | collective-permute-start | bytes 3145736 | tf_op jit(solution)/shard_map/ppermute | solution.py:13
  5.1 3.0 %collective-permute-start.1 = (bf16[2,256,1024]{2,1,0:T(8,128)(2,1)}, bf16[2,256,1024]{2,1,0:T(8,128)(2,1)}, u32[]{:S(2)}, u32[]{:S(2)}) collective-permute-start(bf16[2,256,1024]{2,1,0:T(8,128)(2,1)} %param.12), channel_id=1, source_target_pairs={{0,2},{2,4},{4,6},{6,8},{8,10},{10,12},{12,14},{14,16},{16,18},{18... | collective-permute-start | bytes 3145736 | tf_op jit(solution)/shard_map/ppermute | solution.py:13
  8.1 2.3 %collective-permute-start.2 = (bf16[2,256,1024]{2,1,0:T(8,128)(2,1)}, bf16[2,256,1024]{2,1,0:T(8,128)(2,1)}, u32[]{:S(2)}, u32[]{:S(2)}) collective-permute-start(bf16[2,256,1024]{2,1,0:T(8,128)(2,1)} %param.12), channel_id=1, source_target_pairs={{2,0},{4,2},{6,4},{8,6},{10,8},{12,10},{14,12},{16,14},{18,16},{20... | collective-permute-start | bytes 3145736 | tf_op jit(solution)/shard_map/ppermute | solution.py:13
  11.7 6.5 %fusion.22 = bf16[2,256,3072]{2,1,0:T(8,128)(2,1)S(1)} fusion(bf16[2,256,1024]{2,1,0:T(8,128)(2,1)} %param.12, bf16[1024,3072]{1,0:T(8,128)(2,1)} %param.15), kind=kOutput, calls=%fused_computation.29 | convolution fusion | flops 3222798336 | bytes 10485760 | tf_op jit(solution)/shard_map/spd,de->spe/dot_general | solution.py:68
  21.0 38.9 %collective-permute-done = bf16[2,256,1024]{2,1,0:T(8,128)(2,1)} collective-permute-done((bf16[2,256,1024]{2,1,0:T(8,128)(2,1)}, bf16[2,256,1024]{2,1,0:T(8,128)(2,1)}, u32[]{:S(2)}, u32[]{:S(2)}) %collective-permute-start) | collective-permute-done | bytes 1048608 | tf_op jit(solution)/shard_map/ppermute | solution.py:13
  59.9 5.0 %fusion.36 = bf16[2,1280,2048]{2,1,0:T(8,128)(2,1)S(1)} fusion(bf16[2,256,1024]{2,1,0:T(8,128)(2,1)} %collective-permute-done, bf16[1024,3072]{1,0:T(8,128)(2,1)} %param.15), kind=kOutput, calls=%fused_computation.39 | convolution fusion | flops 2148532224 | bytes 7340032 | tf_op jit(solution)/shard_map/spd,de->spe/dot_general | solution.py:82
  65.0 7.3 %collective-permute-done.1 = bf16[2,256,1024]{2,1,0:T(8,128)(2,1)} collective-permute-done((bf16[2,256,1024]{2,1,0:T(8,128)(2,1)}, bf16[2,256,1024]{2,1,0:T(8,128)(2,1)}, u32[]{:S(2)}, u32[]{:S(2)}) %collective-permute-start.1) | collective-permute-done | bytes 1048608 | tf_op jit(solution)/shard_map/ppermute | solution.py:13
  72.3 4.8 %fusion.42 = bf16[2,1280,2048]{2,1,0:T(8,128)(2,1)S(1)} fusion(bf16[2,1280,2048]{2,1,0:T(8,128)(2,1)S(1)} %fusion.36, bf16[2,256,1024]{2,1,0:T(8,128)(2,1)} %collective-permute-done.1, bf16[1024,3072]{1,0:T(8,128)(2,1)} %param.15), kind=kOutput, calls=%fused_computation.41 | convolution fusion | flops 2148532224 | bytes 7340032 | tf_op jit(solution)/shard_map/spd,de->spe/dot_general | solution.py:82
  77.4 3.6 %fusion.48 = bf16[2,1280,2048]{2,1,0:T(8,128)(2,1)S(1)} fusion(bf16[2,1280,2048]{2,1,0:T(8,128)(2,1)S(1)} %slice_dynamic-update-slice_fusion, bf16[2,256,1024]{2,1,0:T(8,128)(2,1)} %collective-permute-done.2, bf16[1024,3072]{1,0:T(8,128)(2,1)S(1)} %bitcast.119), kind=kOutput, calls=%fused_computation.43 | convolution fusion | flops 2148532224 | bytes 7340032 | tf_op jit(solution)/shard_map/spd,de->spe/dot_general | solution.py:87
  81.0 2.3 %fusion.54 = bf16[2,1280,2048]{2,1,0:T(8,128)(2,1)S(1)} fusion(bf16[2,1280,2048]{2,1,0:T(8,128)(2,1)S(1)} %fusion.48, bf16[2,256,1024]{2,1,0:T(8,128)(2,1)S(1)} %collective-permute-done.3, bf16[1024,3072]{1,0:T(8,128)(2,1)S(1)} %bitcast.119), kind=kOutput, calls=%fused_computation.45 | convolution fusion | flops 2148532224 | bytes 7340032 | tf_op jit(solution)/shard_map/spd,de->spe/dot_general | solution.py:87
  83.3 4.0 %copy-done.1 = bf16[2,1280,2048]{2,1,0:T(8,128)(2,1)} copy-done((bf16[2,1280,2048]{2,1,0:T(8,128)(2,1)}, bf16[2,1280,2048]{2,1,0:T(8,128)(2,1)S(1)}, u32[]{:S(2)}) %copy-start.1) | copy-done | bytes 10485784
  87.3 121.8 %while.33 = (s32[]{:T(128)}, bf16[2,256,1024]{1,2,0:T(8,128)(2,1)}, s32[]{:T(128)}, s32[2]{0:T(128)S(1)}, bf16[2,256,1024]{2,1,0:T(8,128)(2,1)}, /*index=5*/bf16...) while((s32[]{:T(128)}, bf16[2,256,1024]{1,2,0:T(8,128)(2,1)}, ...), condition=%wide.region_5.6_spmd, body=%wide.region_0.5_spmd.sunk | while | flops 348394496 | bytes 47223572 | solution.py:103
  88.5 5.6 %constant_dynamic-slice_fusion.9 = bf16[1,1280,2048]{2,1,0:T(8,128)(2,1)} fusion(bf16[2,1280,2048]{2,1,0:T(8,128)(2,1)} %get-tuple-element.537, s32[]{:T(128)} %get-tuple-element.513), kind=kLoop, calls=%fused_computation.25.clone.1 | loop fusion | bytes 10485764 | tf_op jit(solution)/shard_map/while/body/jit(dynamic_index_in_dim)/dynamic_slice | solution.py:103
  94.1 7.9 %copy.31 = bf16[1,1280,2048]{1,2,0:T(8,128)(2,1)} copy(bf16[1,1280,2048]{2,1,0:T(8,128)(2,1)} %constant_dynamic-slice_fusion.9) | data formatting | bytes 10485760 | tf_op jit(solution)/shard_map/while/body/jit(dynamic_index_in_dim)/dynamic_slice | solution.py:103
  104.6 41.6 %while.34 = (s32[]{:T(128)}, bf16[4,256,256]{1,2,0:T(8,128)(2,1)}, s32[4]{0:T(128)}, bf16[1280,2048]{0,1:T(8,128)(2,1)}, s32[16]{0:T(128)}, /*index=5*/bf16[256,...) while((s32[]{:T(128)}, bf16[4,256,256]{1,2,0:T(8,128)(2,1)}, ...), condition=%wide.region_4.4_spmd.clone, body=%wide.region_1.3_spmd.clone.sunk | while | flops 348130304 | bytes 23098768 | solution.py:58
  146.3 1.9 fusion.93
  149.4 5.6 %constant_dynamic-slice_fusion.9 = bf16[1,1280,2048]{2,1,0:T(8,128)(2,1)} fusion(bf16[2,1280,2048]{2,1,0:T(8,128)(2,1)} %get-tuple-element.537, s32[]{:T(128)} %get-tuple-element.513), kind=kLoop, calls=%fused_computation.25.clone.1 | loop fusion | bytes 10485764 | tf_op jit(solution)/shard_map/while/body/jit(dynamic_index_in_dim)/dynamic_slice | solution.py:103
  155.0 7.9 %copy.31 = bf16[1,1280,2048]{1,2,0:T(8,128)(2,1)} copy(bf16[1,1280,2048]{2,1,0:T(8,128)(2,1)} %constant_dynamic-slice_fusion.9) | data formatting | bytes 10485760 | tf_op jit(solution)/shard_map/while/body/jit(dynamic_index_in_dim)/dynamic_slice | solution.py:103
  165.5 41.6 %while.34 = (s32[]{:T(128)}, bf16[4,256,256]{1,2,0:T(8,128)(2,1)}, s32[4]{0:T(128)}, bf16[1280,2048]{0,1:T(8,128)(2,1)}, s32[16]{0:T(128)}, /*index=5*/bf16[256,...) while((s32[]{:T(128)}, bf16[4,256,256]{1,2,0:T(8,128)(2,1)}, ...), condition=%wide.region_4.4_spmd.clone, body=%wide.region_1.3_spmd.clone.sunk | while | flops 348130304 | bytes 23098768 | solution.py:58
  207.2 1.9 fusion.93
  209.1 2.9 %add_convert_fusion.1 = bf16[2,256,1024]{2,1,0:T(8,128)(2,1)S(1)} fusion(bf16[2,256,1024]{2,1,0:T(8,128)(2,1)} %param.12, bf16[2,256,1024]{1,2,0:T(8,128)(2,1)} %get-tuple-element.223, bf16[1024,1024]{1,0:T(8,128)(2,1)S(1)} %copy-done), kind=kOutput, calls=%fused_computation.54 | convolution fusion | flops 1075314688 | bytes 5242880 | tf_op jit(solution)/shard_map/spd,de->spe/dot_general | solution.py:106
  215.7 1.8 fusion.71
  217.5 6.8 %collective-permute-done.4 = bf16[2,256,512]{2,1,0:T(8,128)(2,1)} collective-permute-done((bf16[2,256,512]{2,1,0:T(8,128)(2,1)}, bf16[2,256,512]{2,1,0:T(8,128)(2,1)}, u32[]{:S(2)}, u32[]{:S(2)}) %collective-permute-start.4) | collective-permute-done | bytes 524320 | tf_op jit(solution)/shard_map/ppermute | solution.py:117
  226.2 3.0 %add_convert_fusion = bf16[2,256,1024]{2,1,0:T(8,128)(2,1)} fusion(bf16[2,256,1024]{2,1,0:T(8,128)(2,1)} %copy-done.5, bf16[512,1024]{1,0:T(8,128)(2,1)S(1)} %copy-done.4, f32[2,256,512]{2,0,1:T(2,128)S(1)} %fusion.69, f32[2,256,512]{2,0,1:T(2,128)S(1)} %fusion.71), kind=kOutput, calls=%fused_computation.53 | convolution fusion | flops 538968064 | bytes 5242880 | tf_op jit(solution)/shard_map/spc,cd->spd/dot_general | solution.py:127
  (127 shorter events, 88.2 us)
Async XLA Ops:
  0.0 209.1 %copy-start = (bf16[1024,1024]{1,0:T(8,128)(2,1)S(1)}, bf16[1024,1024]{1,0:T(8,128)(2,1)}, u32[]{:S(2)}) copy-start(bf16[1024,1024]{1,0:T(8,128)(2,1)} %param.16) | copy-start | bytes 6291460
  0.0 59.9 %collective-permute-start = (bf16[2,256,1024]{2,1,0:T(8,128)(2,1)}, bf16[2,256,1024]{2,1,0:T(8,128)(2,1)}, u32[]{:S(2)}, u32[]{:S(2)}) collective-permute-start(bf16[2,256,1024]{2,1,0:T(8,128)(2,1)} %param.12), channel_id=1, source_target_pairs={{0,4},{2,6},{4,8},{6,10},{8,12},{10,14},{12,16},{14,18},{16,20},{1... | collective-permute-start | bytes 3145736 | tf_op jit(solution)/shard_map/ppermute | solution.py:13
  5.1 67.2 %collective-permute-start.1 = (bf16[2,256,1024]{2,1,0:T(8,128)(2,1)}, bf16[2,256,1024]{2,1,0:T(8,128)(2,1)}, u32[]{:S(2)}, u32[]{:S(2)}) collective-permute-start(bf16[2,256,1024]{2,1,0:T(8,128)(2,1)} %param.12), channel_id=1, source_target_pairs={{0,2},{2,4},{4,6},{6,8},{8,10},{10,12},{12,14},{14,16},{16,18},{18... | collective-permute-start | bytes 3145736 | tf_op jit(solution)/shard_map/ppermute | solution.py:13
  8.1 69.3 %collective-permute-start.2 = (bf16[2,256,1024]{2,1,0:T(8,128)(2,1)}, bf16[2,256,1024]{2,1,0:T(8,128)(2,1)}, u32[]{:S(2)}, u32[]{:S(2)}) collective-permute-start(bf16[2,256,1024]{2,1,0:T(8,128)(2,1)} %param.12), channel_id=1, source_target_pairs={{2,0},{4,2},{6,4},{8,6},{10,8},{12,10},{14,12},{16,14},{18,16},{20... | collective-permute-start | bytes 3145736 | tf_op jit(solution)/shard_map/ppermute | solution.py:13
  10.4 70.6 %collective-permute-start.3 = (bf16[2,256,1024]{2,1,0:T(8,128)(2,1)}, bf16[2,256,1024]{2,1,0:T(8,128)(2,1)S(1)}, u32[]{:S(2)}, u32[]{:S(2)}) collective-permute-start(bf16[2,256,1024]{2,1,0:T(8,128)(2,1)} %param.12), channel_id=1, source_target_pairs={{4,0},{6,2},{8,4},{10,6},{12,8},{14,10},{16,12},{18,14},{20,16},{2... | collective-permute-start | bytes 3145736 | tf_op jit(solution)/shard_map/ppermute | solution.py:13
  18.3 1.7 copy-start.2
  59.9 17.4 %slice-start = ((s8[6291456]{0:T(1024)(128)(4,1)}), s8[4194304]{0:T(1024)(128)(4,1)S(1)}, s32[]{:S(2)}) async-start(s8[6291456]{0:T(1024)(128)(4,1)} %bitcast.118), calls=%async_computation | async-start | bytes 8388608
  64.9 12.2 %copy-start.3 = (bf16[2,256,3072]{2,1,0:T(8,128)(2,1)S(1)}, bf16[2,256,3072]{2,1,0:T(8,128)(2,1)}, u32[]{:S(2)}) copy-start(bf16[2,256,3072]{2,1,0:T(8,128)(2,1)} %copy-done.2) | copy-start | bytes 9437188
  65.0 12.4 %slice-start.1 = ((s8[6291456]{0:T(1024)(128)(4,1)}), s8[2097152]{0:T(1024)(128)(4,1)S(1)}, s32[]{:S(2)}) async-start(s8[6291456]{0:T(1024)(128)(4,1)} %bitcast.118), calls=%async_computation.1 | async-start | bytes 4194304
  81.0 6.3 %copy-start.8 = (s32[2]{0:T(128)S(1)}, s32[2]{0:T(128)}, u32[]{:S(2)}) copy-start(s32[2]{0:T(128)} %param.13) | copy-start | bytes 28
  83.3 4.0 %copy-start.1 = (bf16[2,1280,2048]{2,1,0:T(8,128)(2,1)}, bf16[2,1280,2048]{2,1,0:T(8,128)(2,1)S(1)}, u32[]{:S(2)}) copy-start(bf16[2,1280,2048]{2,1,0:T(8,128)(2,1)S(1)} %fusion.54) | copy-start | bytes 31457284
  209.1 3.9 %copy-start.6 = (bf16[1024,512]{1,0:T(8,128)(2,1)S(1)}, bf16[1024,512]{1,0:T(8,128)(2,1)}, u32[]{:S(2)}) copy-start(bf16[1024,512]{1,0:T(8,128)(2,1)} %param.17) | copy-start | bytes 3145732
  209.1 6.6 %copy-start.7 = (bf16[4,4]{1,0:T(4,128)(2,1)S(1)}, bf16[4,4]{1,0:T(4,128)(2,1)}, u32[]{:S(2)}) copy-start(bf16[4,4]{1,0:T(4,128)(2,1)} %param.19) | copy-start | bytes 100
  212.0 1.0 copy-start.5
  213.0 13.2 %copy-start.4 = (bf16[512,1024]{1,0:T(8,128)(2,1)S(1)}, bf16[512,1024]{1,0:T(8,128)(2,1)}, u32[]{:S(2)}) copy-start(bf16[512,1024]{1,0:T(8,128)(2,1)} %param.18) | copy-start | bytes 3145732
  214.5 9.9 %collective-permute-start.4 = (bf16[2,256,512]{2,1,0:T(8,128)(2,1)}, bf16[2,256,512]{2,1,0:T(8,128)(2,1)}, u32[]{:S(2)}, u32[]{:S(2)}) collective-permute-start(bf16[2,256,512]{2,1,0:T(8,128)(2,1)} %convolution_convert_fusion), channel_id=1, source_target_pairs={{0,1},{1,0},{2,3},{3,2},{4,5},{5,4},{6,7},{7,6},{8,9},{9,8},{10,11... | collective-permute-start | bytes 1572872 | tf_op jit(solution)/shard_map/ppermute | solution.py:117
